TPU v7x, 32 devices: a whole 2x2x4 slice. The times are simulated.
32 devices in a mesh: fsdp: 16 (over z, y, x), dp: 2 (over core).
Axes of the slice: x: 2, y: 2, z: 4, core: 2. Of those that a mesh axis runs over, the one named last changes fastest.
Arguments:
- tokens: bfloat16 [32, 1024, 768], P(('fsdp', 'dp')), may hold values from -6 to 6
- lengths: int32 [32], P(('fsdp', 'dp')), may hold values from 512 to 1024, as said below
- first_gain: bfloat16 [768], P('fsdp'), may hold values from 0.099609375 to 1.8984375
- first_bias: bfloat16 [768], P('fsdp'), may hold values from -3 to 3
- qkv_weight: bfloat16 [768, 2304], P('fsdp'), may hold values from -0.21875 to 0.21875
- qkv_bias: bfloat16 [2304], P('fsdp'), may hold values from -3 to 3
- out_weight: bfloat16 [768, 768], P('fsdp'), may hold values from -6 to 6
- out_bias: bfloat16 [768], P('fsdp'), may hold values from -3 to 3
- second_gain: bfloat16 [768], P('fsdp'), may hold values from 0.099609375 to 1.8984375
- second_bias: bfloat16 [768], P('fsdp'), may hold values from -3 to 3
- up_weight: bfloat16 [768, 3072], P('fsdp'), may hold values from -0.21875 to 0.21875
- up_bias: bfloat16 [3072], P('fsdp'), may hold values from -3 to 3
- down_weight: bfloat16 [3072, 768], P('fsdp'), may hold values from -0.109375 to 0.109375
- down_bias: bfloat16 [768], P('fsdp'), may hold values from -3 to 3
- cotangent: bfloat16 [32, 1024, 768], P(('fsdp', 'dp')), may hold values from -6 to 6
Outputs:
- block_output: bfloat16 [32, 1024, 768], P(('fsdp', 'dp'))
- input_grad: bfloat16 [32, 1024, 768], P(('fsdp', 'dp'))
- first_gain_grad: float32 [768], P('fsdp')
- first_bias_grad: float32 [768], P('fsdp')
- qkv_weight_grad: float32 [768, 2304], P('fsdp')
- qkv_bias_grad: float32 [2304], P('fsdp')
- out_weight_grad: float32 [768, 768], P('fsdp')
- out_bias_grad: float32 [768], P('fsdp')
- second_gain_grad: float32 [768], P('fsdp')
- second_bias_grad: float32 [768], P('fsdp')
- up_weight_grad: float32 [768, 3072], P('fsdp')
- up_bias_grad: float32 [3072], P('fsdp')
- down_weight_grad: float32 [3072, 768], P('fsdp')
- down_bias_grad: float32 [768], P('fsdp')
Inputs may be any that keep to these rules, and one draw needn't show every extreme that they name: `lengths`: each sequence holds 1024 or 512 codons; the first holds 1024.
All inputs are finite; a program needn't handle non-finite values.
Results may differ from a plain program's by a relative error of at most 0.012.
The roundings to bfloat16 on the way count: a program that leaves them out, or rounds other values in their place, can miss the bound.
Values may be sent and summed in bfloat16 or wider, within the bound.
A program may use at most 256 MiB of HBM per device.

v0:
```python
from functools import partial

import jax
import jax.numpy as jnp
from jax import lax
from jax.sharding import PartitionSpec as P

HEADS = 12


EPSILON = 1e-05


def layer_norm(values, gain_vec, shift_vec):
    center = values - jnp.mean(values, axis=-1, keepdims=True)
    inv_scale = lax.rsqrt(jnp.mean(center * center, axis=-1, keepdims=True) + EPSILON)
    return center * inv_scale * gain_vec + shift_vec


def rotary_tables(seq_length, head_size):
    half_size = head_size // 2
    inverse = jnp.exp(
        -jnp.log(10000.0) * jnp.arange(half_size, dtype=jnp.float32) * 2.0 / head_size
    )
    angles = jnp.arange(seq_length, dtype=jnp.float32)[:, None] * inverse[None, :]
    return (jnp.cos(angles), jnp.sin(angles))


def rotate(values, cosine_table, sine_table):
    half_size = values.shape[-1] // 2
    front_half = values[..., :half_size]
    back_half = values[..., half_size:]
    cos_wide = cosine_table[:, None, :]
    sin_wide = sine_table[:, None, :]
    return jnp.concatenate(
        [
            front_half * cos_wide - back_half * sin_wide,
            back_half * cos_wide + front_half * sin_wide,
        ],
        axis=-1,
    )


def local(
    tokens,
    lengths,
    first_gain,
    first_bias,
    qkv_weight,
    qkv_bias,
    out_weight,
    out_bias,
    second_gain,
    second_bias,
    up_weight,
    up_bias,
    down_weight,
    down_bias,
    cotangent,
):
    seq_count, seq_length, model_width = tokens.shape
    head_count = HEADS
    head_size = model_width // head_count
    token_rows = seq_count * seq_length
    score_scale = head_size ** (-0.5)
    block_rows = min(512, seq_length)
    block_count = seq_length // block_rows
    f32 = jnp.float32
    b16 = jnp.bfloat16
    gain_one, shift_one, qkv_full, qkv_shift, out_full, out_shift = (
        lax.all_gather(first_gain, "fsdp", axis=0, tiled=True),
        lax.all_gather(first_bias, "fsdp", axis=0, tiled=True),
        lax.all_gather(qkv_weight, "fsdp", axis=0, tiled=True),
        lax.all_gather(qkv_bias, "fsdp", axis=0, tiled=True),
        lax.all_gather(out_weight, "fsdp", axis=0, tiled=True),
        lax.all_gather(out_bias, "fsdp", axis=0, tiled=True),
    )
    inputs_flat = tokens.reshape(token_rows, model_width).astype(f32)
    normed, first_pull = jax.vjp(
        layer_norm, inputs_flat, gain_one.astype(f32), shift_one.astype(f32)
    )
    normed_low = normed.astype(b16)
    projected = jnp.dot(normed_low, qkv_full, preferred_element_type=f32) + qkv_shift.astype(f32)
    projected = projected.reshape(seq_count, seq_length, 3, head_count, head_size)
    cosine_table, sine_table = rotary_tables(seq_length, head_size)
    queries = rotate(projected[:, :, 0], cosine_table, sine_table).astype(b16)
    key_heads = rotate(projected[:, :, 1], cosine_table, sine_table).astype(b16)
    value_heads = projected[:, :, 2].astype(b16)
    positions = jnp.arange(seq_length, dtype=jnp.int32)
    key_mask = positions[None, :] < lengths[:, None]
    query_blocks = jnp.moveaxis(
        queries.reshape(seq_count, block_count, block_rows, head_count, head_size), 1, 0
    )

    def block_scores(query_block):
        scores = (
            jnp.einsum("sqhd,skhd->shqk", query_block, key_heads, preferred_element_type=f32)
            * score_scale
        )
        return jnp.where(key_mask[:, None, None, :], scores, -1e30)

    def forward_block(query_block):
        scores = block_scores(query_block)
        highest = jnp.max(scores, axis=-1, keepdims=True)
        exponent = jnp.exp(scores - highest)
        summed = jnp.sum(exponent, axis=-1, keepdims=True)
        probability = exponent / summed
        attended_block = jnp.einsum(
            "shqk,skhd->sqhd", probability.astype(b16), value_heads, preferred_element_type=f32
        )
        return (attended_block, (highest + jnp.log(summed))[..., 0])

    attended, log_sums = lax.map(forward_block, query_blocks)
    attended = jnp.moveaxis(attended, 0, 1).reshape(token_rows, model_width).astype(b16)
    middle = (
        inputs_flat
        + jnp.dot(attended, out_full, preferred_element_type=f32)
        + out_shift.astype(f32)
    )
    gain_two, shift_two, up_full, up_shift, down_full, down_shift = (
        lax.all_gather(second_gain, "fsdp", axis=0, tiled=True),
        lax.all_gather(second_bias, "fsdp", axis=0, tiled=True),
        lax.all_gather(up_weight, "fsdp", axis=0, tiled=True),
        lax.all_gather(up_bias, "fsdp", axis=0, tiled=True),
        lax.all_gather(down_weight, "fsdp", axis=0, tiled=True),
        lax.all_gather(down_bias, "fsdp", axis=0, tiled=True),
    )
    second_normed, second_pull = jax.vjp(
        layer_norm, middle, gain_two.astype(f32), shift_two.astype(f32)
    )
    second_low = second_normed.astype(b16)
    pre_active = jnp.dot(second_low, up_full, preferred_element_type=f32) + up_shift.astype(f32)
    activated, gelu_pull = jax.vjp(partial(jax.nn.gelu, approximate=False), pre_active)
    active_low = activated.astype(b16)
    result = (
        middle + jnp.dot(active_low, down_full, preferred_element_type=f32) + down_shift.astype(f32)
    )
    block_output = result.astype(b16).reshape(seq_count, seq_length, model_width)
    qkv_mat, out_mat, up_mat, down_mat = (
        lax.all_gather(qkv_weight, "fsdp", axis=0, tiled=True),
        lax.all_gather(out_weight, "fsdp", axis=0, tiled=True),
        lax.all_gather(up_weight, "fsdp", axis=0, tiled=True),
        lax.all_gather(down_weight, "fsdp", axis=0, tiled=True),
    )
    valid_rows = key_mask.reshape(token_rows, 1).astype(f32)
    grad_result = cotangent.reshape(token_rows, model_width).astype(f32) * valid_rows
    grad_result_low = grad_result.astype(b16)
    down_bias_grad = jnp.sum(grad_result, axis=0)
    down_weight_grad = jnp.einsum(
        "tf,to->fo", active_low, grad_result_low, preferred_element_type=f32
    )
    grad_active = jnp.einsum("to,fo->tf", grad_result_low, down_mat, preferred_element_type=f32)
    (grad_pre,) = gelu_pull(grad_active)
    up_bias_grad = jnp.sum(grad_pre, axis=0)
    grad_pre_low = grad_pre.astype(b16)
    up_weight_grad = jnp.einsum("ti,tf->if", second_low, grad_pre_low, preferred_element_type=f32)
    grad_second = jnp.einsum("tf,if->ti", grad_pre_low, up_mat, preferred_element_type=f32)
    grad_middle_norm, second_gain_grad, second_bias_grad = second_pull(grad_second)
    grad_middle = grad_result + grad_middle_norm
    out_bias_grad = jnp.sum(grad_middle, axis=0)
    grad_middle_low = grad_middle.astype(b16)
    out_weight_grad = jnp.einsum("ti,to->io", attended, grad_middle_low, preferred_element_type=f32)
    grad_attended = jnp.einsum(
        "to,io->ti", grad_middle_low, out_mat, preferred_element_type=f32
    ).astype(b16)
    grad_blocks = jnp.moveaxis(
        grad_attended.reshape(seq_count, block_count, block_rows, head_count, head_size), 1, 0
    )

    def backward_block(running, entries):
        grad_keys, grad_values = running
        query_block, grad_block, log_block = entries
        probability = jnp.exp(block_scores(query_block) - log_block[..., None])
        grad_probs = jnp.einsum(
            "sqhd,skhd->shqk", grad_block, value_heads, preferred_element_type=f32
        )
        inner_sum = jnp.sum(grad_probs * probability, axis=-1, keepdims=True)
        grad_scores = (probability * (grad_probs - inner_sum) * score_scale).astype(b16)
        grad_queries = jnp.einsum(
            "shqk,skhd->sqhd", grad_scores, key_heads, preferred_element_type=f32
        )
        grad_keys = grad_keys + jnp.einsum(
            "shqk,sqhd->skhd", grad_scores, query_block, preferred_element_type=f32
        )
        grad_values = grad_values + jnp.einsum(
            "shqk,sqhd->skhd", probability.astype(b16), grad_block, preferred_element_type=f32
        )
        return ((grad_keys, grad_values), grad_queries)

    zero_heads = jnp.zeros((seq_count, seq_length, head_count, head_size), f32)
    (grad_keys, grad_values), grad_queries = lax.scan(
        backward_block, (zero_heads, zero_heads), (query_blocks, grad_blocks, log_sums)
    )
    grad_queries = jnp.moveaxis(grad_queries, 0, 1).reshape(
        seq_count, seq_length, head_count, head_size
    )
    grad_mixed = jnp.stack(
        [
            rotate(grad_queries, cosine_table, -sine_table),
            rotate(grad_keys, cosine_table, -sine_table),
            grad_values,
        ],
        axis=2,
    ).reshape(token_rows, 3 * model_width)
    qkv_bias_grad = jnp.sum(grad_mixed, axis=0)
    grad_mixed_low = grad_mixed.astype(b16)
    qkv_weight_grad = jnp.einsum(
        "ti,tj->ij", normed_low, grad_mixed_low, preferred_element_type=f32
    )
    grad_normed = jnp.einsum("tj,ij->ti", grad_mixed_low, qkv_mat, preferred_element_type=f32)
    grad_input_norm, first_gain_grad, first_bias_grad = first_pull(grad_normed)
    input_grad = (
        (grad_middle + grad_input_norm).astype(b16).reshape(seq_count, seq_length, model_width)
    )
    row_sums = (
        lax.psum_scatter(first_gain_grad, "fsdp", scatter_dimension=0, tiled=True),
        lax.psum_scatter(first_bias_grad, "fsdp", scatter_dimension=0, tiled=True),
        lax.psum_scatter(qkv_weight_grad, "fsdp", scatter_dimension=0, tiled=True),
        lax.psum_scatter(qkv_bias_grad, "fsdp", scatter_dimension=0, tiled=True),
        lax.psum_scatter(out_weight_grad, "fsdp", scatter_dimension=0, tiled=True),
        lax.psum_scatter(out_bias_grad, "fsdp", scatter_dimension=0, tiled=True),
        lax.psum_scatter(second_gain_grad, "fsdp", scatter_dimension=0, tiled=True),
        lax.psum_scatter(second_bias_grad, "fsdp", scatter_dimension=0, tiled=True),
        lax.psum_scatter(up_weight_grad, "fsdp", scatter_dimension=0, tiled=True),
        lax.psum_scatter(up_bias_grad, "fsdp", scatter_dimension=0, tiled=True),
        lax.psum_scatter(down_weight_grad, "fsdp", scatter_dimension=0, tiled=True),
        lax.psum_scatter(down_bias_grad, "fsdp", scatter_dimension=0, tiled=True),
    )
    (
        gain_one_sum,
        bias_one_sum,
        qkv_w_sum,
        qkv_b_sum,
        out_w_sum,
        out_b_sum,
        gain_two_sum,
        bias_two_sum,
        up_w_sum,
        up_b_sum,
        down_w_sum,
        down_b_sum,
    ) = row_sums
    final_grads = (
        lax.psum(gain_one_sum.astype(jnp.bfloat16), "dp").astype(jnp.float32),
        lax.psum(bias_one_sum.astype(jnp.bfloat16), "dp").astype(jnp.float32),
        lax.psum(qkv_w_sum.astype(jnp.bfloat16), "dp").astype(jnp.float32),
        lax.psum(qkv_b_sum.astype(jnp.bfloat16), "dp").astype(jnp.float32),
        lax.psum(out_w_sum.astype(jnp.bfloat16), "dp").astype(jnp.float32),
        lax.psum(out_b_sum.astype(jnp.bfloat16), "dp").astype(jnp.float32),
        lax.psum(gain_two_sum.astype(jnp.bfloat16), "dp").astype(jnp.float32),
        lax.psum(bias_two_sum.astype(jnp.bfloat16), "dp").astype(jnp.float32),
        lax.psum(up_w_sum.astype(jnp.bfloat16), "dp").astype(jnp.float32),
        lax.psum(up_b_sum.astype(jnp.bfloat16), "dp").astype(jnp.float32),
        lax.psum(down_w_sum.astype(jnp.bfloat16), "dp").astype(jnp.float32),
        lax.psum(down_b_sum.astype(jnp.bfloat16), "dp").astype(jnp.float32),
    )
    return (
        block_output,
        input_grad,
        final_grads[0],
        final_grads[1],
        final_grads[2],
        final_grads[3],
        final_grads[4],
        final_grads[5],
        final_grads[6],
        final_grads[7],
        final_grads[8],
        final_grads[9],
        final_grads[10],
        final_grads[11],
    )


def solution(mesh):
    return jax.shard_map(
        local,
        mesh=mesh,
        in_specs=(
            P(("fsdp", "dp"), None, None),
            P(("fsdp", "dp")),
            P("fsdp"),
            P("fsdp"),
            P("fsdp", None),
            P("fsdp"),
            P("fsdp", None),
            P("fsdp"),
            P("fsdp"),
            P("fsdp"),
            P("fsdp", None),
            P("fsdp"),
            P("fsdp", None),
            P("fsdp"),
            P(("fsdp", "dp"), None, None),
        ),
        out_specs=(
            P(("fsdp", "dp"), None, None),
            P(("fsdp", "dp"), None, None),
            P("fsdp"),
            P("fsdp"),
            P("fsdp", None),
            P("fsdp"),
            P("fsdp", None),
            P("fsdp"),
            P("fsdp"),
            P("fsdp"),
            P("fsdp", None),
            P("fsdp"),
            P("fsdp", None),
            P("fsdp"),
        ),
        check_vma=False,
    )
```

profile of v0, /device:TPU:0, one launch (start us, length us, event | category | flops | bytes accessed | tf_op | source)
XLA Modules:
  0.0 1333.1 jit_solution(6736092482124867917)
XLA Ops:
  21.3 80.0 %all-reduce.17 = (bf16[768]{0:T(1024)(128)(2,1)}, bf16[2304]{0:T(1024)(128)(2,1)S(1)}, bf16[768]{0:T(1024)(128)(2,1)S(1)}, bf16[768]{0:T(1024)(128)(2,1)S(1)}, b...) all-reduce(bf16[768]{0:T(1024)(128)(2,1)S(1)} %dynamic-update-slice, ...), channel_id=1, replica_groups=mesh['fsdp'=16,'dp'=2] {'fsdp'}, use_global_device_ids=true, to_apply=%add.7 | all-reduce | flops 9984 | bytes 39936
  109.8 8.6 convolution_add_fusion
  118.5 9.6 copy.61
  136.3 73.2 %while.28 = (s32[]{:T(128)}, bf16[2,1,512,12,64]{2,4,3,1,0:T(8,128)(2,1)}, f32[2,1,12,512]{3,2,1,0:T(8,128)S(1)}, bf16[2,1,512,12,64]{2,4,3,1,0:T(8,128)(2,1)}, ...) while((s32[]{:T(128)}, ...), condition=%wide.region_5.6_spmd.clone, body=%wide.region_2.5_spmd.clone.sunk | while | flops 1686105088 | bytes 93827240 | solution.py:113
  137.4 11.7 fusion.171
  149.1 11.5 fusion.172
  160.6 11.2 bitcast_dynamic-update-slice_fusion.6
  173.6 11.8 fusion.171
  185.4 11.7 fusion.172
  197.1 11.2 bitcast_dynamic-update-slice_fusion.6
  214.1 3.9 fusion.134
  220.1 3.7 all-gather.9.cloned.1.call-done
  223.8 37.9 %multiply_convert_fusion.1 = (bf16[1024,3072]{1,0:T(8,128)(2,1)}, f32[1024,3072]{1,0:T(8,128)}, f32[1024,3072]{1,0:T(8,128)}) fusion(f32[3072]{0:T(1024)S(1)} %copy-done.41, bf16[768,3072]{1,0:T(8,128)(2,1)} %all-gather.9.cloned.1.call-done, f32[1024,768]{0,1:T(8,128)} %copy-done.2, f32[768]{0:T(1024)S(1)} %copy-done.44, f32[768]{0:T(1024)S(1)} %copy-done.28, ...), kind=kOutput, calls=%fused_computation.61 | convolution fusion | flops 5043388416 | bytes 39348224 | tf_op jit(solution)/shard_map/dot_general | solution.py:132
  261.6 43.0 %all-gather.11.cloned.1.call-done = bf16[3072,768]{1,0:T(8,128)(2,1)} async-done(((bf16[192,768]{1,0:T(8,128)(2,1)}), bf16[3072,768]{1,0:T(8,128)(2,1)}) %all-gather.11.cloned.1.call-update) | async-done | bytes 4718608 | tf_op jit(solution)/shard_map/all_gather | solution.py:125
  304.7 19.4 %fusion.137 = (f32[3072]{0:T(1024)}, bf16[1024,3072]{1,0:T(8,128)(2,1)}) fusion(f32[1024,3072]{1,0:T(8,128)} %get-tuple-element.305, bf16[3072,768]{1,0:T(8,128)(2,1)} %all-gather.11.cloned.1.call-done, bf16[1,1024,768]{1,2,0:T(8,128)(2,1)} %copy.66, f32[1024]{0:T(1024)S(1)} %copy-done.39, f32[1024,3072]{1,0:T(8,128)} %get-tuple-element.330, ...), kind=kOutput, calls=%fused_computation.183 | convolution fusion | flops 4884526080 | bytes 37777408 | tf_op jit(solution)/shard_map/to,fo->tf/dot_general | solution.py:152
  324.1 10.3 fusion.136
  334.4 3.5 copy.67
  351.2 4.8 convolution_convert_fusion
  358.7 3.8 transpose_reshape.4
  365.5 332.7 %while.29 = (s32[]{:T(128)}, f32[1,1024,12,64]{1,3,2,0:T(8,128)}, f32[1,1024,12,64]{1,3,2,0:T(8,128)}, f32[2,1,512,12,64]{2,0,4,3,1:T(2,128)}, bf16[2,1,512,12,6...) while((s32[]{:T(128)}, f32[1,1024,12,64]{1,3,2,0:T(8,128)}, ...), condition=%wide.region_12.13_spmd.clone, body=%wide.region_10.12_spmd.clone.sunk | while | flops 4193270784 | bytes 261272768 | solution.py:191
  366.4 11.5 fusion.184
  377.9 13.1 bitcast_add_fusion.5
  391.1 10.2 fusion.183
  401.3 50.8 %fusion.185 = f32[1,1,512,12,64]{2,4,3,1,0:T(8,128)} fusion(bf16[1,1024,12,64]{1,3,2,0:T(8,128)(2,1)S(1)} %get-tuple-element.502, f32[12,512,1024]{2,1,0:T(8,128)} %fusion.183, f32[12,512]{1,0:T(8,128)S(1)} %dynamic-slice_bitcast_fusion.2, f32[12,512,1024]{2,1,0:T(8,128)} %fusion.184, pred[1024]{0:T(1024)(128)(4,1)S(1)} %compare_reduce_fusion.5), kind=kOutput, calls=%fused_computation.35.clone.1 | convolution fusion | flops 874519552 | bytes 53502976 | tf_op jit(solution)/shard_map/while/body/eval_jaxpr/shqk,skhd->sqhd/dot_general | solution.py:179
  452.0 46.3 %bitcast_add_fusion.4 = f32[1,1024,12,64]{1,3,2,0:T(8,128)} fusion(f32[1,1024,12,64]{1,3,2,0:T(8,128)} %get-tuple-element.486, f32[12,512,1024]{2,1,0:T(8,128)} %fusion.183, f32[12,512]{1,0:T(8,128)S(1)} %dynamic-slice_bitcast_fusion.2, f32[12,512,1024]{2,1,0:T(8,128)} %fusion.184, pred[1024]{0:T(1024)(128)(4,1)S(1)} %compare_reduce_fusion.5, ...), kind=kOutput, calls=%fused_computation.29.clone.1 | convolution fusion | flops 876092416 | bytes 107808776 | tf_op jit(solution)/shard_map/while/body/eval_jaxpr/shqk,sqhd->skhd/dot_general | solution.py:182
  498.4 4.2 copy.101
  502.5 28.8 %dynamic_update_slice.21 = f32[2,1,512,12,64]{2,0,4,3,1:T(2,128)} dynamic-update-slice(f32[2,1,512,12,64]{2,0,4,3,1:T(2,128)} %get-tuple-element.488, f32[1,1,512,12,64]{2,0,4,3,1:T(1,128)} %copy.101, s32[]{:T(128)S(6)} %copy.127, s32[]{:T(128)} %constant.62.clone.1..sunk, s32[]{:T(128)} %constant.62.clone.1..sunk, s32[]{:T(128)} %constant.62.clone.1..sunk, s32[]{:T(128)} %constant.62.clone.1..sunk) | dynamic-update-slice | bytes 3145732 | tf_op jit(solution)/shard_map/while/body/jit(dynamic_update_index_in_dim)/dynamic_update_slice | solution.py:113
  532.1 11.5 fusion.184
  543.5 13.8 %bitcast_add_fusion.5 = f32[1,1024,12,64]{1,3,2,0:T(8,128)} fusion(f32[1,1024,12,64]{1,3,2,0:T(8,128)} %get-tuple-element.487, f32[12,512]{1,0:T(8,128)S(1)} %dynamic-slice_bitcast_fusion.2, f32[12,512,1024]{2,1,0:T(8,128)} %fusion.184, pred[1024]{0:T(1024)(128)(4,1)S(1)} %compare_reduce_fusion.5, pred[]{:T(512)S(6)} %compare.3, ...), kind=kOutput, calls=%fused_computation.28.clone.1 | convolution fusion | flops 832045056 | bytes 32277508 | tf_op jit(solution)/shard_map/while/body/eval_jaxpr/shqk,sqhd->skhd/dot_general | solution.py:185
  557.3 10.1 fusion.183
  567.4 50.8 %fusion.185 = f32[1,1,512,12,64]{2,4,3,1,0:T(8,128)} fusion(bf16[1,1024,12,64]{1,3,2,0:T(8,128)(2,1)S(1)} %get-tuple-element.502, f32[12,512,1024]{2,1,0:T(8,128)} %fusion.183, f32[12,512]{1,0:T(8,128)S(1)} %dynamic-slice_bitcast_fusion.2, f32[12,512,1024]{2,1,0:T(8,128)} %fusion.184, pred[1024]{0:T(1024)(128)(4,1)S(1)} %compare_reduce_fusion.5), kind=kOutput, calls=%fused_computation.35.clone.1 | convolution fusion | flops 874519552 | bytes 53502976 | tf_op jit(solution)/shard_map/while/body/eval_jaxpr/shqk,skhd->sqhd/dot_general | solution.py:179
  618.1 46.8 %bitcast_add_fusion.4 = f32[1,1024,12,64]{1,3,2,0:T(8,128)} fusion(f32[1,1024,12,64]{1,3,2,0:T(8,128)} %get-tuple-element.486, f32[12,512,1024]{2,1,0:T(8,128)} %fusion.183, f32[12,512]{1,0:T(8,128)S(1)} %dynamic-slice_bitcast_fusion.2, f32[12,512,1024]{2,1,0:T(8,128)} %fusion.184, pred[1024]{0:T(1024)(128)(4,1)S(1)} %compare_reduce_fusion.5, ...), kind=kOutput, calls=%fused_computation.29.clone.1 | convolution fusion | flops 876092416 | bytes 107808776 | tf_op jit(solution)/shard_map/while/body/eval_jaxpr/shqk,sqhd->skhd/dot_general | solution.py:182
  664.9 4.2 copy.101
  669.1 28.8 %dynamic_update_slice.21 = f32[2,1,512,12,64]{2,0,4,3,1:T(2,128)} dynamic-update-slice(f32[2,1,512,12,64]{2,0,4,3,1:T(2,128)} %get-tuple-element.488, f32[1,1,512,12,64]{2,0,4,3,1:T(1,128)} %copy.101, s32[]{:T(128)S(6)} %copy.127, s32[]{:T(128)} %constant.62.clone.1..sunk, s32[]{:T(128)} %constant.62.clone.1..sunk, s32[]{:T(128)} %constant.62.clone.1..sunk, s32[]{:T(128)} %constant.62.clone.1..sunk) | dynamic-update-slice | bytes 3145732 | tf_op jit(solution)/shard_map/while/body/jit(dynamic_update_index_in_dim)/dynamic_update_slice | solution.py:113
  698.3 4.3 reshape_transpose.4
  706.3 4.7 fusion.74
  713.3 6.4 fusion.103
  720.4 10.6 fusion.96
  732.4 10.3 fusion.115
  744.9 9.0 fusion.135
  753.9 3.6 copy.71
  762.1 8.7 fusion.114
  772.4 98.2 %reduce-scatter.5.cloned.1.call-done = f32[48,2304]{1,0:T(8,128)} async-done(((f32[768,2304]{1,0:T(8,128)}), f32[48,2304]{1,0:T(8,128)}) %reduce-scatter.5.cloned.1.call-update) | async-done | bytes 442384 | tf_op jit(solution)/shard_map/reduce_scatter | solution.py:218
  872.4 174.9 %reduce-scatter.9.cloned.1.call-done = f32[48,3072]{1,0:T(8,128)} async-done(((f32[768,3072]{1,0:T(8,128)}), f32[48,3072]{1,0:T(8,128)}) %reduce-scatter.9.cloned.1.call-update) | async-done | bytes 589840 | tf_op jit(solution)/shard_map/reduce_scatter | solution.py:224
  1049.1 174.6 %reduce-scatter.11.cloned.1.call-done = f32[192,768]{1,0:T(8,128)} async-done(((f32[3072,768]{1,0:T(8,128)}), f32[192,768]{1,0:T(8,128)}) %reduce-scatter.11.cloned.1.call-update) | async-done | bytes 589840 | tf_op jit(solution)/shard_map/reduce_scatter | solution.py:226
  1225.5 4.2 fusion.73
  1231.4 75.3 %all-reduce.16 = (bf16[768]{0:T(1024)(128)(2,1)S(1)}, bf16[768]{0:T(1024)(128)(2,1)S(1)}, bf16[2304]{0:T(1024)(128)(2,1)S(1)}, bf16[768]{0:T(1024)(128)(2,1)S(1)...) all-reduce(f32[768]{0:T(1024)S(1)} %get-tuple-element.238, ...), channel_id=2, replica_groups=mesh['fsdp'=16,'dp'=2] {'fsdp'}, use_global_device_ids=true, to_apply=%region_16.17.clone | all-reduce | flops 9984 | bytes 59904
  1314.0 3.9 fusion.100
  (228 shorter events, 95.6 us)
Async XLA Ops:
  7.2 102.7 %all-gather.5.cloned.1.call-start = ((), (), s32[]{:S(2)}) async-start(), calls=%async_computation.4 | async-start | bytes 3760128 | tf_op jit(solution)/shard_map/all_gather | solution.py:73
  7.9 206.2 %all-gather.7.cloned.1.call-start = ((), (), s32[]{:S(2)}) async-start(), calls=%async_computation.5 | async-start | bytes 1253376 | tf_op jit(solution)/shard_map/all_gather | solution.py:75
  8.7 215.1 %all-gather.9.cloned.1.call-start = ((), (), s32[]{:S(2)}) async-start(), calls=%async_computation.6 | async-start | bytes 5013504 | tf_op jit(solution)/shard_map/all_gather | solution.py:123
  9.4 295.3 %all-gather.11.cloned.1.call-start = ((), (), s32[]{:S(2)}) async-start(), calls=%async_computation.7 | async-start | bytes 5013504 | tf_op jit(solution)/shard_map/all_gather | solution.py:125
  10.0 760.9 %reduce-scatter.7.cloned.1.call-start = ((), (), s32[]{:S(2)}) async-start(), calls=%async_computation.9 | async-start | bytes 2506752 | tf_op jit(solution)/shard_map/reduce_scatter | solution.py:220
  101.4 8.4 copy-start.26
  102.0 7.8 copy-start.46
  105.0 28.7 %copy-start.19 = (f32[1024,32]{0,1:T(8,128)}, f32[1024,32]{0,1:T(8,128)S(1)}, u32[]{:S(2)}) copy-start(f32[1024,32]{0,1:T(8,128)S(1)} %get-tuple-element.327) | copy-start | bytes 393220
  105.0 3.2 copy-start.15
  106.8 3.0 copy-start
  107.1 11.4 copy-start.22
  108.2 10.3 copy-start.30
  149.1 11.5 copy-start.16
  185.4 11.7 copy-start.16
  209.5 4.6 copy-start.48
  218.0 5.8 copy-start.28
  218.0 5.8 copy-start.41
  218.0 5.8 copy-start.44
  218.0 126.5 %copy-start.24 = (f32[1024]{0:T(1024)}, f32[1024]{0:T(1024)S(1)}, u32[]{:S(2)}) copy-start(f32[1024]{0:T(1024)S(1)} %broadcast_multiply_fusion) | copy-start | bytes 12292
  220.1 124.4 %copy-start.32 = (f32[1024]{0:T(1024)}, f32[1024]{0:T(1024)S(1)}, u32[]{:S(2)}) copy-start(f32[1024]{0:T(1024)S(1)} %fusion.127) | copy-start | bytes 12292
  220.1 84.6 %copy-start.39 = (f32[1024]{0:T(1024)S(1)}, f32[1024]{0:T(1024)}, u32[]{:S(2)}) copy-start(f32[1024]{0:T(1024)} %fusion.125) | copy-start | bytes 12292
  337.9 3.7 copy-start.3
  337.9 4.7 copy-start.6
  342.6 1.9 copy-start.12
  344.5 3.9 copy-start.18
  365.5 505.2 %reduce-scatter.5.cloned.1.call-start = ((), (), s32[]{:S(2)}) async-start(), calls=%async_computation.8 | async-start | bytes 7520256 | tf_op jit(solution)/shard_map/reduce_scatter | solution.py:218
  366.4 11.6 copy-start.10
  532.0 11.5 copy-start.10
  698.2 4.3 copy-start.20
  698.3 4.3 copy-start.21
  706.3 4.8 copy-start.8
  706.3 4.8 copy-start.9
  706.3 7.0 copy-start.1
  706.3 7.0 copy-start.23
  706.3 7.0 copy-start.27
  706.3 7.0 copy-start.31
  706.3 7.0 copy-start.47
  711.0 2.3 copy-start.14
  719.7 327.5 %reduce-scatter.9.cloned.1.call-start = ((), (), s32[]{:S(2)}) async-start(), calls=%async_computation.10 | async-start | bytes 10027008 | tf_op jit(solution)/shard_map/reduce_scatter | solution.py:224
  731.0 492.7 %reduce-scatter.11.cloned.1.call-start = ((), (), s32[]{:S(2)}) async-start(), calls=%async_computation.11 | async-start | bytes 10027008 | tf_op jit(solution)/shard_map/reduce_scatter | solution.py:226
  742.6 2.2 copy-start.49
  742.7 576.8 %all-reduce.22.cloned.1.call-start = ((), (), s32[]{:S(2)}) async-start(), calls=%async_computation.12 | async-start | bytes 1769472 | tf_op jit(solution)/shard_map/psum | solution.py:246
  757.5 2.6 copy-start.35
  757.5 2.9 copy-start.5
  760.1 2.0 copy-start.4
  1229.7 1.7 copy-start.36
  1229.7 1.7 copy-start.37
  1229.7 1.7 copy-start.38
  (14 other events, 16.3 us)
Sparse Core Ops, SparseCore 0:
  10.8 74.2 all-gather.4
  87.8 54.5 all-gather.6
  145.3 78.4 all-gather.8
  226.4 78.2 all-gather.10
  365.6 128.3 reduce-scatter.6
  719.8 150.7 reduce-scatter.4
  876.3 170.8 reduce-scatter.8
  1052.9 170.6 reduce-scatter.10
  1227.4 18.6 all-reduce.21
where the time goes:
time: 1350 us; the launch traced here: 1330 us
  waiting for transfers between devices  497 us (37%)
  matrix products  443 us (33%)
  blocking collectives  158 us (12%)
  local copies, waits for them, and re-layouts  135 us (10%)
  other arithmetic  78.4 us (6%)
  between operations  19.2 us (1%)
    reduce_scatter x1, waiting for transfers between devices, local(): lax.psum_scatter(up_weight_grad, 'fsdp', scatter_dimension=0, tiled=True)  175 us
    reduce_scatter x1, waiting for transfers between devices, local(): lax.psum_scatter(down_weight_grad, 'fsdp', scatter_dimension=0, tiled=True)  175 us
    unnamed x2, blocking collectives  155 us
    dot_general x2, matrix products, backward_block(): jnp.einsum('shqk,skhd->sqhd', grad_scores, key_heads, preferred_element_t...  102 us
    reduce_scatter x1, waiting for transfers between devices, local(): lax.psum_scatter(qkv_weight_grad, 'fsdp', scatter_dimension=0, tiled=True)  98.2 us
    dot_general x2, matrix products, backward_block(): jnp.einsum('shqk,sqhd->skhd', grad_scores, query_block, preferred_element...  93.1 us
    dynamic_update_slice x4, local copies, waits for them, and re-layouts, local(): attended, log_sums = lax.map(forward_block, query_blocks)  66 us
    dot_general x4, matrix products, block_scores(): jnp.einsum('sqhd,skhd->shqk', query_block, key_heads, preferred_element_t...  46.5 us
  transfers between devices with their start and end apart: 9, of which 5 were waited for; matrix products, arithmetic and copies ran while one was open for 43% of the time, Pallas kernels for 0%

commit v1 on v0

v1 whole, which is shorter than its diff:
```python
import functools

import jax
import jax.numpy as jnp
from jax import lax
from jax.experimental import pallas as pl
from jax.experimental.pallas import tpu as pltpu
from jax.sharding import PartitionSpec as P

HEADS = 12
EPSILON = 1e-05
F32 = jnp.float32
B16 = jnp.bfloat16
VMEM_LIMIT = 60 * 1024 * 1024


def params(steps=1, **more):
    return pltpu.CompilerParams(
        dimension_semantics=("arbitrary",) * steps, vmem_limit_bytes=VMEM_LIMIT, **more
    )


def dot_nt(a, b):
    return lax.dot_general(a, b, (((1,), (1,)), ((), ())), preferred_element_type=F32)


def dot_tn(a, b):
    return lax.dot_general(a, b, (((0,), (0,)), ((), ())), preferred_element_type=F32)


def rotary_tables(seq_length, head_size):
    half_size = head_size // 2
    inverse = jnp.exp(
        -jnp.log(10000.0) * jnp.arange(half_size, dtype=F32) * 2.0 / head_size
    )
    angles = jnp.arange(seq_length, dtype=F32)[:, None] * inverse[None, :]
    cosine, sine = jnp.cos(angles), jnp.sin(angles)
    return (
        jnp.concatenate([cosine] * 4, axis=1),
        jnp.concatenate([-sine, sine] * 2, axis=1),
    )


def spin(values, cosine, sine):
    lane = lax.broadcasted_iota(jnp.int32, values.shape, 1)
    partner = jnp.where(
        lane % 64 < 32, pltpu.roll(values, 96, 1), pltpu.roll(values, 32, 1)
    )
    return values * cosine + partner * sine


def qkv_kernel(blocks, x_ref, g_ref, b_ref, w_ref, wb_ref, c_ref, s_ref, a_ref, o_ref):
    step = pl.program_id(0)

    @pl.when(step == 0)
    def _():
        x = x_ref[...].astype(F32)
        center = x - jnp.mean(x, axis=-1, keepdims=True)
        scale = lax.rsqrt(jnp.mean(center * center, axis=-1, keepdims=True) + EPSILON)
        a_ref[...] = (center * scale * g_ref[...] + b_ref[...]).astype(B16)

    out = jnp.dot(a_ref[...], w_ref[...], preferred_element_type=F32) + wb_ref[...]

    @pl.when(step < 2 * blocks)
    def _():
        factor = jnp.where(step < blocks, 0.125, 1.0)
        for part in range(out.shape[1] // 128):
            lanes = slice(part * 128, part * 128 + 128)
            turned = spin(out[:, lanes], c_ref[...], s_ref[...])
            o_ref[:, lanes] = (turned * factor).astype(B16)

    @pl.when(step >= 2 * blocks)
    def _():
        o_ref[...] = out.astype(B16)


def qkv_call(x, gain, bias, weight, weight_bias, cosine, sine):
    rows, width = x.shape
    tile = 256
    blocks = width // tile
    return pl.pallas_call(
        functools.partial(qkv_kernel, blocks),
        grid=(3 * blocks,),
        in_specs=[
            pl.BlockSpec((rows, width), lambda j: (0, 0)),
            pl.BlockSpec((1, width), lambda j: (0, 0)),
            pl.BlockSpec((1, width), lambda j: (0, 0)),
            pl.BlockSpec((width, tile), lambda j: (0, j)),
            pl.BlockSpec((1, tile), lambda j: (0, j)),
            pl.BlockSpec((rows, 128), lambda j: (0, 0)),
            pl.BlockSpec((rows, 128), lambda j: (0, 0)),
        ],
        out_specs=[
            pl.BlockSpec((rows, width), lambda j: (0, 0)),
            pl.BlockSpec((rows, tile), lambda j: (0, j)),
        ],
        out_shape=[
            jax.ShapeDtypeStruct((rows, width), B16),
            jax.ShapeDtypeStruct((rows, 3 * width), B16),
        ],
        compiler_params=params(),
        cost_estimate=pl.CostEstimate(
            flops=2 * rows * width * 3 * width,
            bytes_accessed=2 * (2 * rows * width + 3 * width * width + 3 * rows * width),
            transcendentals=0,
        ),
        name="qkv",
    )(x, gain, bias, weight, weight_bias, cosine, sine)


def head_of(values, head):
    lane = lax.broadcasted_iota(jnp.int32, values.shape, 1)
    return jnp.where(lane // 64 == head, values, jnp.zeros_like(values))


QUERY_ROWS = 256


def attend_kernel(n_ref, q_ref, k_ref, v_ref, o_ref, l_ref):
    rows = q_ref.shape[0]

    def run(keys):
        k, v = k_ref[:keys, :], v_ref[:keys, :]
        for at in range(0, rows, QUERY_ROWS):
            q = q_ref[at : at + QUERY_ROWS, :]
            halves = []
            for head in range(2):
                scores = dot_nt(head_of(k, head), q)
                top = jnp.max(scores, axis=0, keepdims=True)
                weight = jnp.exp(scores - top)
                total = jnp.sum(weight, axis=0, keepdims=True)
                mixed = dot_tn(v, weight.astype(B16)) / total
                halves.append(mixed[head * 64 : head * 64 + 64, :])
                l_ref[0, head : head + 1, at : at + QUERY_ROWS] = top + jnp.log(total)
            o_ref[at : at + QUERY_ROWS, :] = jnp.concatenate(halves, axis=0).T.astype(B16)

    full = n_ref[0] == rows
    pl.when(full)(lambda: run(rows))
    pl.when(jnp.logical_not(full))(lambda: run(rows // 2))


def attend_call(lengths, packed):
    rows, width = packed.shape[0], packed.shape[1] // 3
    pairs = width // 128
    return pl.pallas_call(
        attend_kernel,
        grid_spec=pltpu.PrefetchScalarGridSpec(
            num_scalar_prefetch=1,
            grid=(pairs,),
            in_specs=[
                pl.BlockSpec((rows, 128), lambda j, n: (0, j)),
                pl.BlockSpec((rows, 128), lambda j, n: (0, pairs + j)),
                pl.BlockSpec((rows, 128), lambda j, n: (0, 2 * pairs + j)),
            ],
            out_specs=[
                pl.BlockSpec((rows, 128), lambda j, n: (0, j)),
                pl.BlockSpec((1, 2, rows), lambda j, n: (j, 0, 0)),
            ],
        ),
        out_shape=[
            jax.ShapeDtypeStruct((rows, width), B16),
            jax.ShapeDtypeStruct((pairs, 2, rows), F32),
        ],
        compiler_params=params(),
        cost_estimate=pl.CostEstimate(
            flops=16 * rows * rows * width,
            bytes_accessed=8 * rows * width,
            transcendentals=rows * rows * width // 64,
        ),
        name="attend",
    )(lengths, packed, packed, packed)


def attend_back_kernel(
    n_ref, q_ref, k_ref, v_ref, g_ref, l_ref, c_ref, s_ref, dq_ref, dk_ref, dv_ref, db_ref,
    dk_sum, dv_sum,
):
    rows = q_ref.shape[0]

    def run(keys):
        k, v = k_ref[:keys, :], v_ref[:keys, :]
        dk_sum[...] = jnp.zeros_like(dk_sum)
        dv_sum[...] = jnp.zeros_like(dv_sum)
        bias = jnp.zeros((1, 128), F32)
        for at in range(0, keys, QUERY_ROWS):
            span = slice(at, at + QUERY_ROWS)
            q, g = q_ref[span, :], g_ref[span, :]
            turned = None
            for head in range(2):
                k_head = head_of(k, head)
                weight = jnp.exp(dot_nt(k_head, q) - l_ref[0, head : head + 1, span])
                slope = dot_nt(head_of(v, head), g)
                inner = jnp.sum(weight * slope, axis=0, keepdims=True)
                change = (weight * (slope - inner)).astype(B16)
                dk_sum[:keys, :] += jnp.dot(
                    change, head_of(q, head), preferred_element_type=F32
                )
                dv_sum[:keys, :] += jnp.dot(
                    weight.astype(B16), head_of(g, head), preferred_element_type=F32
                )
                part = dot_tn(k_head, change)
                turned = part if turned is None else turned + part
            grad = spin(turned.T * 0.125, c_ref[span, :], -s_ref[span, :])
            bias = bias + jnp.sum(grad, axis=0, keepdims=True)
            dq_ref[span, :] = grad.astype(B16)
        if keys < rows:
            dq_ref[keys:, :] = jnp.zeros((rows - keys, 128), B16)
        dk = spin(dk_sum[...], c_ref[...], -s_ref[...])
        dk_ref[...] = dk.astype(B16)
        dv_ref[...] = dv_sum[...].astype(B16)
        db_ref[0, 0:1, :] = bias
        db_ref[0, 1:2, :] = jnp.sum(dk, axis=0, keepdims=True)
        db_ref[0, 2:3, :] = jnp.sum(dv_sum[...], axis=0, keepdims=True)

    full = n_ref[0] == rows
    pl.when(full)(lambda: run(rows))
    pl.when(jnp.logical_not(full))(lambda: run(rows // 2))


def attend_back_call(lengths, packed, grad, log_sums, cosine, sine):
    rows, width = grad.shape
    pairs = width // 128
    column = pl.BlockSpec((rows, 128), lambda j, n: (0, j))
    return pl.pallas_call(
        attend_back_kernel,
        grid_spec=pltpu.PrefetchScalarGridSpec(
            num_scalar_prefetch=1,
            grid=(pairs,),
            in_specs=[
                column,
                pl.BlockSpec((rows, 128), lambda j, n: (0, pairs + j)),
                pl.BlockSpec((rows, 128), lambda j, n: (0, 2 * pairs + j)),
                column,
                pl.BlockSpec((1, 2, rows), lambda j, n: (j, 0, 0)),
                pl.BlockSpec((rows, 128), lambda j, n: (0, 0)),
                pl.BlockSpec((rows, 128), lambda j, n: (0, 0)),
            ],
            out_specs=[
                column,
                column,
                column,
                pl.BlockSpec((1, 3, 128), lambda j, n: (j, 0, 0)),
            ],
            scratch_shapes=[pltpu.VMEM((rows, 128), F32), pltpu.VMEM((rows, 128), F32)],
        ),
        out_shape=[jax.ShapeDtypeStruct((rows, width), B16)] * 3
        + [jax.ShapeDtypeStruct((pairs, 3, 128), F32)],
        compiler_params=params(),
        cost_estimate=pl.CostEstimate(
            flops=40 * rows * rows * width,
            bytes_accessed=14 * rows * width,
            transcendentals=rows * rows * width // 64,
        ),
        name="attend_back",
    )(lengths, packed, packed, packed, grad, log_sums, cosine, sine)


def norm_parts(values):
    center = values - jnp.mean(values, axis=-1, keepdims=True)
    inverse = lax.rsqrt(jnp.mean(center * center, axis=-1, keepdims=True) + EPSILON)
    return center * inverse, inverse


def norm_back(grad, unit, inverse, gain):
    scaled = grad * gain
    return inverse * (
        scaled
        - jnp.mean(scaled, axis=-1, keepdims=True)
        - unit * jnp.mean(scaled * unit, axis=-1, keepdims=True)
    )


def gather_rows(shard):
    half = shard.shape[1] // 2
    mine = lax.dynamic_slice_in_dim(shard, lax.axis_index("dp") * half, half, axis=1)
    both = lax.all_gather(mine, ("fsdp", "dp"), axis=0, tiled=False)
    ranks, rows = both.shape[0] // 2, both.shape[1]
    both = both.reshape(ranks, 2, rows, half)
    return jnp.moveaxis(both, 1, 2).reshape(ranks * rows, 2 * half)


def scatter_rows(grad, ranks):
    rows, half = grad.shape[0] // ranks, grad.shape[1] // 2
    split = jnp.moveaxis(grad.astype(B16).reshape(ranks, rows, 2, half), 2, 1)
    mine = lax.psum_scatter(
        split.reshape(ranks * 2, rows, half), ("fsdp", "dp"), scatter_dimension=0, tiled=True
    )[0]
    both = lax.all_gather(mine, "dp", axis=0, tiled=False)
    return jnp.moveaxis(both, 0, 1).reshape(rows, 2 * half).astype(F32)


def local(
    ranks,
    tokens,
    lengths,
    first_gain,
    first_bias,
    qkv_weight,
    qkv_bias,
    out_weight,
    out_bias,
    second_gain,
    second_bias,
    up_weight,
    up_bias,
    down_weight,
    down_bias,
    cotangent,
):
    seq_length, model_width = tokens.shape[1:]
    vectors = (
        first_gain, first_bias, qkv_bias, out_bias, second_gain, second_bias, up_bias, down_bias,
    )
    sizes = [v.shape[0] for v in vectors]
    small = lax.all_gather(jnp.concatenate(vectors), "fsdp", axis=0, tiled=False)
    full_vectors, at = [], 0
    for size in sizes:
        full_vectors.append(small[:, at : at + size].reshape(1, -1).astype(F32))
        at += size
    gain_one, shift_one, qkv_shift, out_shift, gain_two, shift_two, up_shift, down_shift = (
        full_vectors
    )
    qkv_full = gather_rows(qkv_weight)
    out_full = gather_rows(out_weight)
    up_full = gather_rows(up_weight)
    down_full = gather_rows(down_weight)
    cosine, sine = rotary_tables(seq_length, model_width // HEADS)

    x = tokens[0]
    a1, packed = qkv_call(x, gain_one, shift_one, qkv_full, qkv_shift, cosine, sine)
    attended, log_sums = attend_call(lengths, packed)

    middle = x.astype(F32) + jnp.dot(attended, out_full, preferred_element_type=F32) + out_shift
    unit_two, inverse_two = norm_parts(middle)
    a2 = (unit_two * gain_two + shift_two).astype(B16)
    pre = jnp.dot(a2, up_full, preferred_element_type=F32) + up_shift
    active, gelu_pull = jax.vjp(functools.partial(jax.nn.gelu, approximate=False), pre)
    active_low = active.astype(B16)
    block_output = (
        middle + jnp.dot(active_low, down_full, preferred_element_type=F32) + down_shift
    ).astype(B16)

    valid = (jnp.arange(seq_length, dtype=jnp.int32) < lengths[0]).astype(F32)[:, None]
    grad_result = cotangent[0].astype(F32) * valid
    grad_low = grad_result.astype(B16)
    down_weight_grad = dot_tn(active_low, grad_low)
    (grad_pre,) = gelu_pull(dot_nt(grad_low, down_full))
    grad_pre_low = grad_pre.astype(B16)
    up_weight_grad = dot_tn(a2, grad_pre_low)
    grad_second = dot_nt(grad_pre_low, up_full)
    grad_middle = grad_result + norm_back(grad_second, unit_two, inverse_two, gain_two)
    grad_middle_low = grad_middle.astype(B16)
    out_weight_grad = dot_tn(attended, grad_middle_low)
    grad_attended = dot_nt(grad_middle_low, out_full).astype(B16)
    dq, dk, dv, mixed_sums = attend_back_call(
        lengths, packed, grad_attended, log_sums, cosine, sine
    )
    grad_mixed = jnp.concatenate([dq, dk, dv], axis=1)
    qkv_weight_grad = dot_tn(a1, grad_mixed)
    grad_normed = dot_nt(grad_mixed, qkv_full)
    unit_one, inverse_one = norm_parts(x.astype(F32))
    input_grad = (grad_middle + norm_back(grad_normed, unit_one, inverse_one, gain_one)).astype(B16)

    sums = (
        jnp.sum(grad_normed * unit_one, axis=0),
        jnp.sum(grad_normed, axis=0),
        jnp.moveaxis(mixed_sums, 1, 0).reshape(-1),
        jnp.sum(grad_middle, axis=0),
        jnp.sum(grad_second * unit_two, axis=0),
        jnp.sum(grad_second, axis=0),
        jnp.sum(grad_pre, axis=0),
        jnp.sum(grad_result, axis=0),
    )
    small_sums = jnp.concatenate([s.reshape(ranks, -1) for s in sums], axis=1)
    small_sums = lax.psum(
        lax.psum_scatter(small_sums, "fsdp", scatter_dimension=0, tiled=True)[0], "dp"
    )
    kept, at = [], 0
    for size in sizes:
        kept.append(small_sums[at : at + size])
        at += size
    return (
        block_output[None],
        input_grad[None],
        kept[0],
        kept[1],
        scatter_rows(qkv_weight_grad, ranks),
        kept[2],
        scatter_rows(out_weight_grad, ranks),
        kept[3],
        kept[4],
        kept[5],
        scatter_rows(up_weight_grad, ranks),
        kept[6],
        scatter_rows(down_weight_grad, ranks),
        kept[7],
    )


def solution(mesh):
    matrix, vector, rows = P("fsdp", None), P("fsdp"), P(("fsdp", "dp"), None, None)
    weights = (
        vector, vector, matrix, vector, matrix, vector,
        vector, vector, matrix, vector, matrix, vector,
    )
    return jax.shard_map(
        functools.partial(local, mesh.shape["fsdp"]),
        mesh=mesh,
        in_specs=(rows, P(("fsdp", "dp"))) + weights + (rows,),
        out_specs=(rows, rows) + weights,
        check_vma=False,
    )
```

time: 1350 us -> 799 us (0.59)
  matrix products: 443 us -> 115 us
  waiting for transfers between devices: 497 us -> 265 us
  Pallas kernels: 0 us -> 98.7 us
  other arithmetic: 78.4 us -> 12.6 us
  local copies, waits for them, and re-layouts: 135 us -> 118 us
    dot_general x26 -> x11, matrix products: 443 us -> 115 us  [the longest x4 40.1 us: dot_nt(): lax.dot_general(a, b, (((1,), (1,)), ((), ())), preferred_element_type=F32)]
    reduce_scatter x4, waiting for transfers between devices: 448 us -> 192 us  [scatter_rows(): lax.psum_scatter(split.reshape(ranks * 2, rows, half), ('fsdp', 'dp'), sc...]
    pallas_call x0 -> x3, Pallas kernels: none -> 98.7 us  [the longest x1 46.4 us: attend_back_call(): pl.pallas_call(attend_back_kernel, grid_spec=pltpu.PrefetchScalarGridSpec...]
    reshape x0 -> x19, local copies, waits for them, and re-layouts: none -> 77.7 us  [the longest x8 51.3 us: scatter_rows(): split = jnp.moveaxis(grad.astype(B16).reshape(ranks, rows, 2, half), 2, 1)]
    dynamic_update_slice x4 -> x0, local copies, waits for them, and re-layouts: 66 us -> none  [local(): attended, log_sums = lax.map(forward_block, query_blocks)]
    reduce_sum x11 -> x4, other arithmetic: 40 us -> 3.08 us  [the longest x1 1.69 us: local(): jnp.sum(grad_middle, axis=0)]
    all_gather x4, waiting for transfers between devices: 46.7 us -> 72.8 us  [gather_rows(): both = lax.all_gather(mine, ('fsdp', 'dp'), axis=0, tiled=False)]
    convert_element_type x26 -> x4, other arithmetic: 25.7 us -> 0.75 us  [the longest x3 0.75 us: local(): full_vectors.append(small[:, at:at + size].reshape(1, -1).astype(F32))]
  transfers between devices with their start and end apart: 9 -> 8, of which waited for: 5 -> 5; matrix products, arithmetic and copies ran while one was open for 43% -> 19% of each run, Pallas kernels for 0% -> 12%
where the time goes in v1:
time: 799 us; the launch traced here: 790 us
  waiting for transfers between devices  265 us (33%)
  blocking collectives  164 us (21%)
  local copies, waits for them, and re-layouts  118 us (15%)
  matrix products  115 us (14%)
  Pallas kernels  98.7 us (12%)
  between operations  16.1 us (2%)
  other arithmetic  12.6 us (2%)
    reduce_scatter x4, waiting for transfers between devices, scatter_rows(): lax.psum_scatter(split.reshape(ranks * 2, rows, half), ('fsdp', 'dp'), sc...  192 us
    unnamed x2, blocking collectives  153 us
    all_gather x4, waiting for transfers between devices, gather_rows(): both = lax.all_gather(mine, ('fsdp', 'dp'), axis=0, tiled=False)  72.8 us
    reshape x8, local copies, waits for them, and re-layouts, scatter_rows(): split = jnp.moveaxis(grad.astype(B16).reshape(ranks, rows, 2, half), 2, 1)  51.3 us
    pallas_call x1, Pallas kernels, attend_back_call(): pl.pallas_call(attend_back_kernel, grid_spec=pltpu.PrefetchScalarGridSpec...  46.4 us
    dot_general x4, matrix products, dot_nt(): lax.dot_general(a, b, (((1,), (1,)), ((), ())), preferred_element_type=F32)  40.1 us
    pallas_call x1, Pallas kernels, attend_call(): pl.pallas_call(attend_kernel, grid_spec=pltpu.PrefetchScalarGridSpec(num_...  38.1 us
    dot_general x1, matrix products, local(): pre = jnp.dot(a2, up_full, preferred_element_type=F32) + up_shift  35.2 us
  transfers between devices with their start and end apart: 8, of which 5 were waited for; matrix products, arithmetic and copies ran while one was open for 19% of the time, Pallas kernels for 12%

profile of v1, /device:TPU:0, one launch (start us, length us, event | category | flops | bytes accessed | tf_op | source)
XLA Modules:
  0.0 789.8 jit_solution(8694209435234946582)
XLA Ops:
  15.4 5.4 concatenate.15
  21.1 79.0 %all-reduce = bf16[9984]{0:T(1024)(128)(2,1)S(1)} all-reduce(bf16[9984]{0:T(1024)(128)(2,1)S(1)} %dynamic-update-slice), channel_id=2, replica_groups=mesh['fsdp'=16,'dp'=2] {'fsdp'}, use_global_device_ids=true, to_apply=%add | all-reduce | flops 9984 | bytes 39936
  103.4 2.0 fusion.38
  105.3 1.8 pad_maximum_fusion
  107.2 2.2 copy.56
  109.6 21.0 %all-gather.10.cloned.1.call-done = bf16[1536,1152]{1,0:T(8,128)(2,1)} async-done(((bf16[48,1152]{1,0:T(8,128)(2,1)}), bf16[1536,1152]{1,0:T(8,128)(2,1)}) %all-gather.10.cloned.1.call-update) | async-done | bytes 3538960 | tf_op jit(solution)/shard_map/all_gather | solution.py:276
  130.6 4.7 copy.55
  135.3 2.5 copy.74
  137.8 14.2 %qkv.1 = (bf16[1024,768]{1,0:T(8,128)(2,1)}, bf16[1024,2304]{1,0:T(8,128)(2,1)}) custom-call(bf16[1024,768]{1,0:T(8,128)(2,1)} %bitcast.103, f32[1,768]{1,0:T(1,128)} %reshape.290.g_ref, f32[1,768]{1,0:T(1,128)} %reshape.291.b_ref, bf16[768,2304]{1,0:T(8,128)(2,1)} %bitcast.112, f32[1,2304]{1,0:T(1,128)} %reshape.292.wb_ref, ...), custom_call_target="tpu_custom_call" | custom-call | flops 3623878656 | bytes 11403264 | tf_op jit(solution)/shard_map/qkv/pallas_call | solution.py:81
  152.0 38.1 %attend.1 = (bf16[1024,768]{1,0:T(8,128)(2,1)}, f32[6,2,1024]{2,1,0:T(2,128)}) custom-call(s32[1]{0:T(128)} %copy.81.n_ref, bf16[1024,2304]{1,0:T(8,128)(2,1)} %get-tuple-element.22.q_ref.k_ref.v_ref, bf16[1024,2304]{1,0:T(8,128)(2,1)} %get-tuple-element.22.q_ref.k_ref.v_ref, bf16[1024,2304]{1,0:T(8,128)(2,1)} %get-tuple-element.22.q_ref.k_ref.v_ref), custom_call_target="tpu_custom_call" | custom-call | flops 12884901888 | bytes 6291456 | tf_op jit(solution)/shard_map/attend/pallas_call | solution.py:145
  190.1 3.0 fusion.46
  193.1 1.6 copy-done.4
  196.5 9.4 %copy.59 = bf16[16,2,192,384]{3,1,2,0:T(2,128)(2,1)} copy(bf16[16,2,192,384]{3,2,1,0:T(8,128)(2,1)} %bitcast.106) | data formatting | bytes 9437184 | tf_op jit(solution)/shard_map/reshape | solution.py:278
  205.9 5.4 copy.77
  211.3 50.5 %all-gather.14.cloned.1.call-done = bf16[1536,1536]{1,0:T(8,128)(2,1)} async-done(((bf16[48,1536]{1,0:T(8,128)(2,1)}), bf16[1536,1536]{1,0:T(8,128)(2,1)}) %all-gather.14.cloned.1.call-update) | async-done | bytes 4718608 | tf_op jit(solution)/shard_map/all_gather | solution.py:276
  261.8 9.5 %copy.58 = bf16[16,2,48,1536]{3,1,2,0:T(2,128)(2,1)} copy(bf16[16,2,48,1536]{3,2,1,0:T(8,128)(2,1)} %bitcast.107) | data formatting | bytes 9437184 | tf_op jit(solution)/shard_map/reshape | solution.py:278
  271.3 3.7 copy.76
  275.0 35.2 %multiply_convert_fusion = (bf16[1024,3072]{1,0:T(8,128)(2,1)}, f32[1024,3072]{1,0:T(8,128)}, f32[1024,3072]{1,0:T(8,128)}) fusion(f32[3072]{0:T(1024)S(1)} %reshape.296, bf16[768,3072]{1,0:T(8,128)(2,1)S(1)} %bitcast.108, f32[1024,768]{1,0:T(8,128)S(1)} %copy-done.5, f32[768]{0:T(1024)S(1)} %reshape.295, f32[768]{0:T(1024)S(1)} %reshape.294, ...), kind=kOutput, calls=%fused_computation.3 | convolution fusion | flops 5043388416 | bytes 39348224 | tf_op jit(solution)/shard_map/dot_general | solution.py:336
  310.2 18.7 %fusion.47 = (f32[3072]{0:T(1024)S(1)}, bf16[1024,3072]{1,0:T(8,128)(2,1)}) fusion(f32[1024,3072]{1,0:T(8,128)} %get-tuple-element.41, bf16[3072,768]{1,0:T(8,128)(2,1)} %bitcast.104, bf16[1,1024,768]{2,1,0:T(8,128)(2,1)} %param.29, f32[1024]{0:T(1024)S(1)} %fusion.39, f32[1024,3072]{1,0:T(8,128)} %get-tuple-element.62, f32[3072]{0:T(1024)S(1)} %reshape.296), kind=kOutput, calls=%fused_computation.105 | convolution fusion | flops 4884526080 | bytes 37777408 | tf_op jit(solution)/shard_map/dot_general | solution.py:24
  328.9 9.3 %multiply_reduce_fusion = (f32[768]{0:T(1024)S(1)}, f32[1024]{0:T(1024)S(1)}, f32[1024]{0:T(1024)S(1)}, f32[768]{0:T(1024)S(1)}, f32[1024,768]{1,0:T(8,128)S(1)}) fusion(f32[1024,768]{1,0:T(8,128)S(1)} %copy-done.5, f32[1024]{0:T(1024)S(1)} %add_rsqrt_fusion.1, f32[1024]{0:T(1024)S(1)} %broadcast_multiply_fusion.5, f32[768]{0:T(1024)S(1)} %reshape.294, ...), kind=kOutput, calls=%fused_computation.43 | convolution fusion | flops 4838912000 | bytes 17327104 | tf_op jit(solution)/shard_map/dot_general | solution.py:24
  338.3 1.7 fusion.41
  340.1 2.5 convolution_convert_fusion.4
  342.6 2.6 convolution_convert_fusion.3.g_ref
  345.2 3.6 reshape.284
  348.8 2.5 copy.63
  351.3 46.4 %attend_back.1 = (bf16[1024,768]{1,0:T(8,128)(2,1)}, bf16[1024,768]{1,0:T(8,128)(2,1)}, bf16[1024,768]{1,0:T(8,128)(2,1)}, f32[6,3,128]{2,1,0:T(4,128)}) custom-call(s32[1]{0:T(128)} %copy.81.n_ref, bf16[1024,2304]{1,0:T(8,128)(2,1)} %get-tuple-element.22.q_ref.k_ref.v_ref, bf16[1024,2304]{1,0:T(8,128)(2,1)} %get-tuple-element.22.q_ref.k_ref.v_ref, ...), custom_call_target="tpu_custom_call" | custom-call | flops 32212254720 | bytes 11010048 | tf_op jit(solution)/shard_map/attend_back/pallas_call | solution.py:224
  397.7 1.7 constant_dynamic-update-slice_fusion.2
  400.2 2.1 copy-done.14
  402.3 5.3 convolution_convert_fusion.2
  407.6 8.2 %reshape.282 = bf16[16,48,2,1152]{3,2,1,0:T(2,128)(2,1)} reshape(bf16[768,2304]{1,0:T(8,128)(2,1)} %convolution_convert_fusion.2) | data formatting | bytes 7077888 | tf_op jit(solution)/shard_map/reshape | solution.py:284
  415.9 4.3 copy.61
  420.2 9.5 %convolution_convert_fusion = bf16[3072,768]{1,0:T(8,128)(2,1)} fusion(bf16[1024,3072]{1,0:T(8,128)(2,1)} %get-tuple-element.40, bf16[1,1024,768]{2,1,0:T(8,128)(2,1)} %param.29, f32[1024]{0:T(1024)S(1)} %fusion.39), kind=kOutput, calls=%fused_computation.17 | convolution fusion | flops 4836556800 | bytes 12587008 | tf_op jit(solution)/shard_map/dot_general | solution.py:28
  429.7 10.1 %reshape.288 = bf16[16,192,2,384]{3,2,1,0:T(2,128)(2,1)} reshape(bf16[3072,768]{1,0:T(8,128)(2,1)} %convolution_convert_fusion) | data formatting | bytes 9437184 | tf_op jit(solution)/shard_map/reshape | solution.py:284
  439.7 5.5 copy.67
  445.3 10.2 %convolution_convert_fusion.1 = bf16[768,3072]{1,0:T(8,128)(2,1)} fusion(bf16[1024,3072]{1,0:T(8,128)(2,1)} %get-tuple-element.66, f32[1024,768]{1,0:T(8,128)S(1)} %copy-done.5, f32[768]{0:T(1024)S(1)} %reshape.295, f32[768]{0:T(1024)S(1)} %reshape.294, f32[1024]{0:T(1024)S(1)} %add_rsqrt_fusion.1, f32[1024]{0:T(1024)S(1)} %broadcast_multiply_fusion.5), kind=kOutput, calls=%fused_computation.18 | convolution fusion | flops 4838129664 | bytes 14170112 | tf_op jit(solution)/shard_map/dot_general | solution.py:28
  455.5 11.7 %reshape.286 = bf16[16,48,2,1536]{3,2,1,0:T(2,128)(2,1)} reshape(bf16[768,3072]{1,0:T(8,128)(2,1)} %convolution_convert_fusion.1) | data formatting | bytes 9437184 | tf_op jit(solution)/shard_map/reshape | solution.py:284
  467.1 5.6 copy.65
  475.6 9.5 %fusion.16 = (f32[768]{0:T(1024)S(1)}, f32[1024]{0:T(1024)S(1)}, f32[1024]{0:T(1024)S(1)}, f32[768]{0:T(1024)S(1)}, f32[1024,768]{1,0:T(8,128)}) fusion(f32[1024]{0:T(1024)S(1)} %add_rsqrt_fusion, f32[1024]{0:T(1024)S(1)} %broadcast_multiply_fusion.2, bf16[1,1024,768]{2,1,0:T(8,128)(2,1)S(1)} %copy-done.3, f32[768]{0:T(1024)S(1)} %reshape.299, ...), kind=kOutput, calls=%fused_computation.35 | convolution fusion | flops 3631739392 | bytes 13001728 | tf_op jit(solution)/shard_map/dot_general | solution.py:24
  485.3 73.7 %all-reduce.1 = f32[16,624]{1,0:T(8,128)S(1)} all-reduce(f32[16,624]{1,0:T(8,128)S(1)} %concatenate.19), channel_id=7, replica_groups=mesh['fsdp'=16,'dp'=2] {'fsdp'}, use_global_device_ids=true, to_apply=%region_15.0.clone | all-reduce | flops 9984 | bytes 79872
  559.7 2.5 psum.7
  564.0 4.8 fusion.30
  568.8 9.6 %fusion.33 = bf16[1,1024,768]{2,1,0:T(8,128)(2,1)} fusion(f32[768]{0:T(1024)S(1)} %reshape.297, f32[1024,768]{1,0:T(8,128)S(1)} %copy-done.6, bf16[1024,3072]{1,0:T(8,128)(2,1)} %get-tuple-element.40, bf16[3072,768]{1,0:T(8,128)(2,1)} %bitcast.105), kind=kOutput, calls=%fused_computation.60 | convolution fusion | flops 4834197504 | bytes 15731712 | tf_op jit(solution)/shard_map/dot_general | solution.py:340
  578.4 2.1 all_gather.53
  581.1 2.2 all_gather.52
  584.1 83.3 %reduce-scatter.11.cloned.1.call-done = bf16[1,192,384]{2,1,0:T(8,128)(2,1)} async-done(((bf16[32,192,384]{2,1,0:T(8,128)(2,1)}), bf16[1,192,384]{2,1,0:T(8,128)(2,1)}) %reduce-scatter.11.cloned.1.call-update) | async-done | bytes 147472 | tf_op jit(solution)/shard_map/reduce_scatter | solution.py:285
  667.4 2.2 all_gather.55
  670.5 109.1 %reduce-scatter.9.cloned.1.call-done = bf16[1,48,1536]{2,1,0:T(8,128)(2,1)} async-done(((bf16[32,48,1536]{2,1,0:T(8,128)(2,1)}), bf16[1,48,1536]{2,1,0:T(8,128)(2,1)}) %reduce-scatter.9.cloned.1.call-update) | async-done | bytes 147472 | tf_op jit(solution)/shard_map/reduce_scatter | solution.py:285
  779.6 2.2 all_gather.54
  (118 shorter events, 22.2 us)
Async XLA Ops:
  7.2 3.2 copy-start
  7.2 100.0 %all-gather.12.cloned.1.call-start = ((), (), s32[]{:S(2)}) async-start(), calls=%async_computation.9 | async-start | bytes 1216512 | tf_op jit(solution)/shard_map/all_gather | solution.py:276
  8.7 121.9 %all-gather.10.cloned.1.call-start = ((), (), s32[]{:S(2)}) async-start(), calls=%async_computation.8 | async-start | bytes 3649536 | tf_op jit(solution)/shard_map/all_gather | solution.py:276
  10.3 186.2 %all-gather.16.cloned.1.call-start = ((), (), s32[]{:S(2)}) async-start(), calls=%async_computation.11 | async-start | bytes 4866048 | tf_op jit(solution)/shard_map/all_gather | solution.py:276
  11.1 250.7 %all-gather.14.cloned.1.call-start = ((), (), s32[]{:S(2)}) async-start(), calls=%async_computation.10 | async-start | bytes 4866048 | tf_op jit(solution)/shard_map/all_gather | solution.py:276
  12.8 565.6 %reduce-scatter.7.cloned.1.call-start = ((), (), s32[]{:S(2)}) async-start(), calls=%async_computation.5 | async-start | bytes 1216512 | tf_op jit(solution)/shard_map/reduce_scatter | solution.py:285
  101.8 7.8 copy-start.15
  109.6 80.5 %copy-start.12 = (bf16[96,8,2,384]{3,1,2,0:T(8,128)(2,1)}, bf16[96,8,2,384]{3,1,2,0:T(8,128)(2,1)S(1)}, u32[]{:S(2)}) copy-start(bf16[96,8,2,384]{3,1,2,0:T(8,128)(2,1)S(1)} %copy.75) | copy-start | bytes 3538948
  152.0 38.1 %copy-start.2 = (bf16[1,1024,768]{2,1,0:T(8,128)(2,1)S(1)}, bf16[1,1024,768]{2,1,0:T(8,128)(2,1)}, u32[]{:S(2)}) copy-start(bf16[1,1024,768]{2,1,0:T(8,128)(2,1)} %param.15) | copy-start | bytes 4718596
  193.1 1.6 copy-start.4
  271.3 3.7 copy-start.5
  275.0 35.2 %copy-start.8 = (bf16[96,8,2,1536]{3,1,2,0:T(8,128)(2,1)}, bf16[96,8,2,1536]{3,1,2,0:T(8,128)(2,1)S(1)}, u32[]{:S(2)}) copy-start(bf16[96,8,2,1536]{3,1,2,0:T(8,128)(2,1)S(1)} %copy.76) | copy-start | bytes 14155780
  328.9 9.4 %copy-start.11 = (bf16[1,1024,768]{2,1,0:T(8,128)(2,1)S(1)}, bf16[1,1024,768]{2,1,0:T(8,128)(2,1)}, u32[]{:S(2)}) copy-start(bf16[1,1024,768]{2,1,0:T(8,128)(2,1)} %param.29) | copy-start | bytes 4718596
  338.3 1.7 copy-start.19
  340.0 2.6 copy-start.7
  340.0 2.6 copy-start.13
  351.2 229.9 %reduce-scatter.5.cloned.1.call-start = ((), (), s32[]{:S(2)}) async-start(), calls=%async_computation.4 | async-start | bytes 3649536 | tf_op jit(solution)/shard_map/reduce_scatter | solution.py:285
  397.7 1.9 copy-start.10
  397.7 2.4 copy-start.9
  399.4 2.9 copy-start.20
  400.2 2.1 copy-start.14
  420.1 247.2 %reduce-scatter.11.cloned.1.call-start = ((), (), s32[]{:S(2)}) async-start(), calls=%async_computation.7 | async-start | bytes 4866048 | tf_op jit(solution)/shard_map/reduce_scatter | solution.py:285
  445.3 334.4 %reduce-scatter.9.cloned.1.call-start = ((), (), s32[]{:S(2)}) async-start(), calls=%async_computation.6 | async-start | bytes 4866048 | tf_op jit(solution)/shard_map/reduce_scatter | solution.py:285
  472.7 0.7 copy-start.16
  472.7 0.8 copy-start.17
  472.7 1.5 copy-start.3
  472.7 2.8 copy-start.18
  564.0 4.8 copy-start.6
  580.4 202.3 %copy-start.1 = (bf16[192,768]{1,0:T(8,128)(2,1)S(1)}, bf16[192,768]{1,0:T(8,128)(2,1)}, u32[]{:S(2)}) copy-start(bf16[192,768]{1,0:T(8,128)(2,1)} %param.27) | copy-start | bytes 884740
Sparse Core Ops, SparseCore 0:
  11.5 56.6 all-gather.11
  71.7 58.8 all-gather.9
  134.1 62.3 all-gather.15
  199.8 61.9 all-gather.13
  351.4 95.3 reduce-scatter.6
  452.1 103.0 reduce-scatter.4
  560.6 106.7 reduce-scatter.10
  672.9 106.6 reduce-scatter.8
